TPU v7x, 32 devices: a whole 2x2x4 slice. The times are simulated.
32 devices in a mesh: owner: 4 (over y, core), rows: 8 (over z, x).
Axes of the slice: x: 2, y: 2, z: 4, core: 2. Of those that a mesh axis runs over, the one named last changes fastest.
Arguments:
- w_gate: float32 [64, 2048, 1024], P('owner', 'rows'), may hold values from -0.1875 to 0.1875
- avg_gate: float32 [64, 2048, 1024], P('owner', 'rows'), may hold values from -0.125 to 0.125
- w_up: float32 [64, 2048, 1024], P('owner', 'rows'), may hold values from -0.1875 to 0.1875
- avg_up: float32 [64, 2048, 1024], P('owner', 'rows'), may hold values from -0.125 to 0.125
- mix_share: float32 [64], P('owner'), may hold values from 0.2 to 0.8
- router_weight: float32 [2048, 64], P('rows', 'owner'), may hold values from -0.125 to 0.125
- router_gain: float32 [2048], P('rows'), may hold values from 0.25 to 1.75
Outputs:
- serve_gate: bfloat16 [64, 2048, 1024], P('owner', None, 'rows')
- serve_up: bfloat16 [64, 2048, 1024], P('owner', None, 'rows')
- scale_gate: float32 [64, 1024], P('owner', 'rows')
- scale_up: float32 [64, 1024], P('owner', 'rows')
- serve_router: bfloat16 [2048, 64], replicated
All inputs are finite; a program needn't handle non-finite values.
Results may differ from a plain program's by a relative error of at most 0.001.
Values may be sent and summed in bfloat16 or wider, within the bound.
No kernel may reach another device: no remote copies, remote signals or barrier semaphores. Data moves between devices by JAX's collectives and lax.ppermute only.
A program may use at most 256 MiB of HBM per device.

v0:
```python
import jax
import jax.numpy as jnp
from jax import lax
from jax.sharding import PartitionSpec as P


def body(w_gate, avg_gate, w_up, avg_up, mix_share, router_weight, router_gain):
    fresh_gate = mix_share[:, None, None] * w_gate + (1.0 - mix_share[:, None, None]) * avg_gate
    fresh_up = mix_share[:, None, None] * w_up + (1.0 - mix_share[:, None, None]) * avg_up
    total_gate, total_up = lax.psum(
        (jnp.sum(fresh_gate * fresh_gate, axis=1), jnp.sum(fresh_up * fresh_up, axis=1)), "rows"
    )
    scale_gate = jnp.sqrt(total_gate)
    scale_up = jnp.sqrt(total_up)
    narrow_gate, narrow_up = (
        (fresh_gate / jnp.expand_dims(scale_gate, 1)).astype(jnp.bfloat16),
        (fresh_up / jnp.expand_dims(scale_up, 1)).astype(jnp.bfloat16),
    )
    serve_gate, serve_up = (
        lax.all_to_all(narrow_gate, "rows", split_axis=2, concat_axis=1, tiled=True),
        lax.all_to_all(narrow_up, "rows", split_axis=2, concat_axis=1, tiled=True),
    )
    scale_gate = lax.dynamic_slice_in_dim(
        scale_gate, lax.axis_index("rows") * serve_gate.shape[2], serve_gate.shape[2], axis=1
    )
    scale_up = lax.dynamic_slice_in_dim(
        scale_up, lax.axis_index("rows") * serve_up.shape[2], serve_up.shape[2], axis=1
    )
    part_router = (router_weight * router_gain[:, None]).astype(jnp.bfloat16)
    row_router = lax.all_gather(part_router, "rows", axis=0, tiled=True)
    serve_router = lax.all_gather(row_router, "owner", axis=1, tiled=True)
    return (serve_gate, serve_up, scale_gate, scale_up, serve_router)


def solution(mesh):
    in_specs = (
        P("owner", "rows", None),
        P("owner", "rows", None),
        P("owner", "rows", None),
        P("owner", "rows", None),
        P("owner"),
        P("rows", "owner"),
        P("rows"),
    )
    out_specs = (
        P("owner", None, "rows"),
        P("owner", None, "rows"),
        P("owner", "rows"),
        P("owner", "rows"),
        P(),
    )
    return jax.shard_map(body, mesh=mesh, in_specs=in_specs, out_specs=out_specs, check_vma=False)
```

profile of v0, /device:TPU:0, one launch (start us, length us, event | category | flops | bytes accessed | tf_op | source)
XLA Modules:
  0.0 643.5 jit_solution(16856830632772673776)
XLA Ops:
  7.2 0.0 copy-start.1
  7.2 0.0 all-reduce.3.cloned.1.call-start
  7.2 17.6 %copy.26 = f32[16,256,1024]{1,0,2:T(8,128)} copy(f32[16,256,1024]{2,1,0:T(8,128)} %param.10) | data formatting | bytes 33554432 | tf_op args[3]
  24.8 0.0 copy-done.1
  24.8 17.6 %copy.25 = f32[16,256,1024]{1,0,2:T(8,128)} copy(f32[16,256,1024]{2,1,0:T(8,128)} %param.9) | data formatting | bytes 33554432 | tf_op args[2]
  42.4 17.6 %copy.23 = f32[16,256,1024]{1,0,2:T(8,128)} copy(f32[16,256,1024]{2,1,0:T(8,128)} %param.8) | data formatting | bytes 33554432 | tf_op args[1]
  60.0 17.6 %copy.22 = f32[16,256,1024]{1,0,2:T(8,128)} copy(f32[16,256,1024]{2,1,0:T(8,128)} %param.7) | data formatting | bytes 33554432 | tf_op args[0]
  77.6 23.8 %multiply_reduce_fusion = (f32[16,1024]{0,1:T(8,128)}, f32[16,1024]{0,1:T(8,128)}) fusion(f32[16,256,1024]{1,0,2:T(8,128)} %copy.26, f32[16]{0:T(128)S(1)} %broadcast_subtract_fusion, f32[16,256,1024]{1,0,2:T(8,128)} %copy.25, f32[16]{0:T(128)S(1)} %copy-done.1, f32[16,256,1024]{1,0,2:T(8,128)} %copy.23, f32[16,256,1024]{1,0,2:T(8,128)} %copy.22), kind=kLoop, calls=%fused_computation.1 | loop fusion | flops 41910272 | bytes 67240064 | tf_op jit(solution)/shard_map/reduce_sum | solution.py:11
  101.4 0.0 all-reduce.3.cloned.1.call-update
  101.4 81.1 %all-reduce.3.cloned.1.call-done = (f32[16,1024]{0,1:T(8,128)}, f32[16,1024]{0,1:T(8,128)}) async-done(((f32[16,1024]{0,1:T(8,128)}, f32[16,1024]{0,1:T(8,128)}), (f32[16,1024]{0,1:T(8,128)}, f32[16,1024]{0,1:T(8,128)})) %all-reduce.3.cloned.1.call-update) | async-done | bytes 131088 | tf_op jit(solution)/shard_map/psum | solution.py:10
  182.6 1.2 sqrt.7
  183.7 1.2 sqrt.6
  184.9 25.3 %divide_convert_fusion = (bf16[16,256,1024]{1,0,2:T(8,128)(2,1)}, bf16[16,256,1024]{1,0,2:T(8,128)(2,1)S(1)}) fusion(f32[16,1024]{0,1:T(8,128)S(1)} %sqrt.7, f32[16,256,1024]{1,0,2:T(8,128)} %copy.26, f32[16]{0:T(128)S(1)} %broadcast_subtract_fusion, f32[16,256,1024]{1,0,2:T(8,128)} %copy.25, f32[16]{0:T(128)S(1)} %copy-done.1, f32[16,1024]{0,1:T(8,128)S(1)} %sqrt.6, ...), kind=kLoop, calls=%fused_computation | loop fusion | flops 41943040 | bytes 84017280 | tf_op jit(solution)/shard_map/convert_element_type | solution.py:17
  210.2 187.0 %all_to_all.36 = bf16[16,256,1024]{1,0,2:T(8,128)(2,1)} all-to-all(bf16[16,256,1024]{1,0,2:T(8,128)(2,1)S(1)} %get-tuple-element.15), channel_id=1, replica_groups=mesh['owner'=4,'rows'=8] {'rows'}, dimensions={2} | all-to-all | bytes 16777216 | tf_op jit(solution)/shard_map/all_to_all | solution.py:20
  397.3 4.9 all-to-all-start.1
  402.2 0.0 copy-done
  402.2 202.0 %all_gather.6 = bf16[2048,16]{0,1:T(8,128)(2,1)S(1)} all-gather(bf16[256,16]{0,1:T(8,128)(2,1)S(1)} %multiply_convert_fusion), channel_id=1, replica_groups=mesh['owner'=4,'rows'=8] {'rows'}, dimensions={0}, use_global_device_ids=true | all-gather | bytes 73728 | tf_op jit(solution)/shard_map/all_gather | solution.py:30
  604.3 5.8 all_gather.7
  610.0 0.7 copy.28
  610.7 0.7 copy.29
  611.4 12.3 %copy.24 = bf16[16,8,256,128]{3,2,1,0:T(8,128)(2,1)} copy(bf16[16,8,256,128]{2,0,3,1:T(8,128)(2,1)} %bitcast.8) | data formatting | bytes 16777216 | tf_op jit(solution)/shard_map/all_to_all | solution.py:20
  623.7 0.0 all-to-all-done.1
  623.7 12.3 %copy.27 = bf16[16,8,256,128]{3,2,1,0:T(8,128)(2,1)} copy(bf16[16,8,256,128]{2,0,3,1:T(8,128)(2,1)} %bitcast.4) | data formatting | bytes 16777216 | tf_op jit(solution)/shard_map/all_to_all | solution.py:21
  635.9 0.7 copy.33
  (6 shorter events, 0.0 us)
Async XLA Ops:
  7.2 17.7 %copy-start.1 = (f32[16]{0:T(128)S(1)}, f32[16]{0:T(128)}, u32[]{:S(2)}) copy-start(f32[16]{0:T(128)} %param.11) | copy-start | bytes 196
  7.2 175.4 %all-reduce.3.cloned.1.call-start = ((), (), s32[]{:S(2)}) async-start(), calls=%async_computation.2 | async-start | bytes 2097152 | tf_op jit(solution)/shard_map/psum | solution.py:10
  210.2 192.0 %copy-start = (f32[256,16]{0,1:T(8,128)S(1)}, f32[256,16]{0,1:T(8,128)}, u32[]{:S(2)}) copy-start(f32[256,16]{0,1:T(8,128)} %param.12) | copy-start | bytes 49156
  210.2 192.0 %copy-start.2 = (f32[256]{0:T(256)S(1)}, f32[256]{0:T(256)}, u32[]{:S(2)}) copy-start(f32[256]{0:T(256)} %param.13) | copy-start | bytes 3076
  397.3 226.4 %all-to-all-start.1 = ((bf16[16,256,1024]{1,0,2:T(8,128)(2,1)}), bf16[16,256,1024]{1,0,2:T(8,128)(2,1)}, u32[]{:S(2)}, u32[]{:S(2)}) async-start(bf16[16,256,1024]{1,0,2:T(8,128)(2,1)} %get-tuple-element.14), calls=%async_computation.1 | async-start | bytes 16777216 | tf_op jit(solution)/shard_map/all_to_all | solution.py:21
Sparse Core Ops, SparseCore 0:
  101.5 80.9 all-reduce.2
where the time goes:
time: 645 us; the launch traced here: 643 us
  blocking collectives  395 us (61%)
  local copies, waits for them, and re-layouts  99.4 us (15%)
  waiting for transfers between devices  81.2 us (13%)
  other arithmetic  49.1 us (8%)
  between operations  14.1 us (2%)
    all_gather x1, blocking collectives, body(): row_router = lax.all_gather(part_router, 'rows', axis=0, tiled=True)  202 us
    all_to_all x1, blocking collectives, body(): lax.all_to_all(narrow_gate, 'rows', split_axis=2, concat_axis=1, tiled=True)  187 us
    psum x1, waiting for transfers between devices, body(): lax.psum((jnp.sum(fresh_gate * fresh_gate, axis=1), jnp.sum(fresh_up * fr...  81.1 us
    unnamed x13, local copies, waits for them, and re-layouts  72.5 us
    convert_element_type x1, other arithmetic, body(): (fresh_up / jnp.expand_dims(scale_up, 1)).astype(jnp.bfloat16)  25.3 us
    reduce_sum x1, other arithmetic, body(): jnp.sum(fresh_up * fresh_up, axis=1)  23.8 us
  transfers between devices with their start and end apart: 2, of which 1 were waited for; matrix products, arithmetic and copies ran while one was open for 2% of the time, Pallas kernels for 0%

commit v1 on v0

v1 whole, which is shorter than its diff:
```python
import jax
import jax.numpy as jnp
from jax import lax
from jax.experimental import pallas as pl
from jax.experimental.pallas import tpu as pltpu
from jax.sharding import PartitionSpec as P

F32 = jnp.float32
BF16 = jnp.bfloat16


def params():
    return pltpu.CompilerParams(dimension_semantics=("arbitrary",), vmem_limit_bytes=48 * 2**20)


def mixed(share_ref, expert, w, avg):
    share = share_ref[expert]
    return share * w + (1.0 - share) * avg


def sums_kernel(share_ref, wg_ref, ag_ref, wu_ref, au_ref, gate_ref, up_ref):
    expert = pl.program_id(0)
    for w_ref, avg_ref, out_ref in ((wg_ref, ag_ref, gate_ref), (wu_ref, au_ref, up_ref)):
        fresh = mixed(share_ref, expert, w_ref[0], avg_ref[0])
        out_ref[0] = jnp.sum(fresh * fresh, axis=0, keepdims=True)


def sums(share, *arrays):
    experts, rows, width = arrays[0].shape
    block = pl.BlockSpec((1, rows, width), lambda e: (e, 0, 0))
    total = pl.BlockSpec((1, 1, width), lambda e: (e, 0, 0))
    return pl.pallas_call(
        sums_kernel,
        grid=(experts,),
        in_specs=[pl.BlockSpec(memory_space=pltpu.SMEM)] + [block] * 4,
        out_specs=[total] * 2,
        out_shape=[jax.ShapeDtypeStruct((experts, 1, width), F32)] * 2,
        compiler_params=params(),
        cost_estimate=pl.CostEstimate(
            flops=10 * experts * rows * width, bytes_accessed=16 * experts * rows * width, transcendentals=0
        ),
        name="sums",
    )(share, *arrays)


def narrow_kernel(share_ref, w_ref, avg_ref, inverse_ref, out_ref):
    expert = pl.program_id(0)
    parts, _, _, columns = out_ref.shape
    for part in range(parts):
        cut = slice(part * columns, (part + 1) * columns)
        fresh = mixed(share_ref, expert, w_ref[0, :, cut], avg_ref[0, :, cut])
        out_ref[part, 0] = (fresh * inverse_ref[0, :, cut]).astype(BF16)


def narrow(share, w, avg, inverse, parts):
    experts, rows, width = w.shape
    columns = width // parts
    block = pl.BlockSpec((1, rows, width), lambda e: (e, 0, 0))
    return pl.pallas_call(
        narrow_kernel,
        grid=(experts,),
        in_specs=[
            pl.BlockSpec(memory_space=pltpu.SMEM),
            block,
            block,
            pl.BlockSpec((1, 1, width), lambda e: (e, 0, 0)),
        ],
        out_specs=pl.BlockSpec((parts, 1, rows, columns), lambda e: (0, e, 0, 0)),
        out_shape=jax.ShapeDtypeStruct((parts, experts, rows, columns), BF16),
        compiler_params=params(),
        cost_estimate=pl.CostEstimate(
            flops=5 * experts * rows * width, bytes_accessed=10 * experts * rows * width, transcendentals=0
        ),
        name="narrow",
    )(share, w, avg, inverse)


def unpack_kernel(in_ref, out_ref):
    parts, _, rows, _ = in_ref.shape
    for part in range(parts):
        out_ref[0, part * rows : (part + 1) * rows] = in_ref[part, 0]


def unpack(arrived):
    parts, experts, rows, columns = arrived.shape
    return pl.pallas_call(
        unpack_kernel,
        grid=(experts,),
        in_specs=[pl.BlockSpec((parts, 1, rows, columns), lambda e: (0, e, 0, 0))],
        out_specs=pl.BlockSpec((1, parts * rows, columns), lambda e: (e, 0, 0)),
        out_shape=jax.ShapeDtypeStruct((experts, parts * rows, columns), BF16),
        compiler_params=params(),
        cost_estimate=pl.CostEstimate(
            flops=arrived.size, bytes_accessed=4 * arrived.size, transcendentals=0
        ),
        name="unpack",
    )(arrived)


def body(parts, w_gate, avg_gate, w_up, avg_up, mix_share, router_weight, router_gain):
    experts, _, width = w_gate.shape
    columns = width // parts

    part_router = (router_weight * router_gain[:, None]).astype(BF16)
    gathered = lax.all_gather(part_router, ("rows", "owner"), axis=0)
    owners = gathered.shape[0] // parts
    router_rows, router_columns = part_router.shape

    partial_gate, partial_up = sums(mix_share, w_gate, avg_gate, w_up, avg_up)
    partial = jnp.concatenate([partial_gate, partial_up]).reshape(2 * experts, parts, columns)
    pieces = lax.all_to_all(partial.transpose(1, 0, 2), "rows", split_axis=0, concat_axis=0, tiled=True)
    scale = jnp.sqrt(jnp.sum(pieces, axis=0))
    scale_gate, scale_up = scale[:experts], scale[experts:]
    inverse = lax.all_gather(1.0 / scale, "rows", axis=0)
    inverse = inverse.transpose(1, 0, 2).reshape(2, experts, 1, width)
    inverse, gathered = lax.optimization_barrier((inverse, gathered))
    serve_router = (
        gathered.reshape(parts, owners, router_rows, router_columns)
        .transpose(0, 2, 1, 3)
        .reshape(parts * router_rows, owners * router_columns)
    )

    def exchange(packed):
        return lax.all_to_all(packed, "rows", split_axis=0, concat_axis=0, tiled=True)

    packed_gate = narrow(mix_share, w_gate, avg_gate, inverse[0], parts)
    arrived_gate = exchange(packed_gate)
    packed_up = narrow(mix_share, w_up, avg_up, inverse[1], parts)
    arrived_up = exchange(packed_up)
    return (unpack(arrived_gate), unpack(arrived_up), scale_gate, scale_up, serve_router)


def solution(mesh):
    parts = mesh.shape["rows"]
    matrix = P("owner", "rows", None)
    in_specs = (matrix, matrix, matrix, matrix, P("owner"), P("rows", "owner"), P("rows"))
    served = P("owner", None, "rows")
    out_specs = (served, served, P("owner", "rows"), P("owner", "rows"), P())

    def step(*arguments):
        return body(parts, *arguments)

    return jax.shard_map(step, mesh=mesh, in_specs=in_specs, out_specs=out_specs, check_vma=False)
```

time: 645 us -> 510 us (0.79)
  blocking collectives: 395 us -> 73.2 us
  waiting for transfers between devices: 81.2 us -> 327 us
  local copies, waits for them, and re-layouts: 99.4 us -> 3.15 us
  Pallas kernels: 0 us -> 86.9 us
  other arithmetic: 49.1 us -> 0.14 us
  between operations: 14.1 us -> 0.76 us
  starting transfers between devices: 4.98 us -> 17.3 us
    all_to_all x1 -> x3, waiting for transfers between devices: 0.01 us -> 327 us  [the longest x2 327 us: exchange(): lax.all_to_all(packed, 'rows', split_axis=0, concat_axis=0, tiled=True)]
    all_to_all x1 -> x0, blocking collectives: 187 us -> none  [body(): lax.all_to_all(narrow_gate, 'rows', split_axis=2, concat_axis=1, tiled=True)]
    all_gather x2, blocking collectives: 208 us -> 73.2 us  [the longest x1 42.7 us: body(): gathered = lax.all_gather(part_router, ('rows', 'owner'), axis=0)]
    pallas_call x0 -> x5, Pallas kernels: none -> 86.9 us  [the longest x2 37.9 us: narrow(): pl.pallas_call(narrow_kernel, grid=(experts,), in_specs=[pl.BlockSpec(mem...]
    psum x1 -> x0, waiting for transfers between devices: 81.1 us -> none  [body(): lax.psum((jnp.sum(fresh_gate * fresh_gate, axis=1), jnp.sum(fresh_up * fr...]
    unnamed x13 -> x10, local copies, waits for them, and re-layouts: 72.5 us -> 1.46 us
    convert_element_type x2 -> x1, other arithmetic: 25.3 us -> 0.01 us  [body(): part_router = (router_weight * router_gain[:, None]).astype(BF16)]
    all_to_all x2 -> x0, local copies, waits for them, and re-layouts: 24.6 us -> none  [the longest x1 12.3 us: body(): lax.all_to_all(narrow_up, 'rows', split_axis=2, concat_axis=1, tiled=True)]
  transfers between devices with their start and end apart: 2 -> 3, of which waited for: 1 -> 2; matrix products, arithmetic and copies ran while one was open for 2% -> 0% of each run, Pallas kernels for 0% -> 6%
where the time goes in v1:
time: 510 us; the launch traced here: 508 us
  waiting for transfers between devices  327 us (64%)
  Pallas kernels  86.9 us (17%)
  blocking collectives  73.2 us (14%)
  starting transfers between devices  17.3 us (3%)
    all_to_all x2, waiting for transfers between devices, exchange(): lax.all_to_all(packed, 'rows', split_axis=0, concat_axis=0, tiled=True)  327 us
    all_gather x1, blocking collectives, body(): gathered = lax.all_gather(part_router, ('rows', 'owner'), axis=0)  42.7 us
    pallas_call x2, Pallas kernels, narrow(): pl.pallas_call(narrow_kernel, grid=(experts,), in_specs=[pl.BlockSpec(mem...  37.9 us
    all_gather x1, blocking collectives, body(): inverse = lax.all_gather(1.0 / scale, 'rows', axis=0)  30.5 us
    pallas_call x1, Pallas kernels, sums(): pl.pallas_call(sums_kernel, grid=(experts,), in_specs=[pl.BlockSpec(memor...  25.3 us
    pallas_call x2, Pallas kernels, unpack(): pl.pallas_call(unpack_kernel, grid=(experts,), in_specs=[pl.BlockSpec((pa...  23.7 us
  transfers between devices with their start and end apart: 3, of which 2 were waited for; matrix products, arithmetic and copies ran while one was open for 0% of the time, Pallas kernels for 6%

profile of v1, /device:TPU:0, one launch (start us, length us, event | category | flops | bytes accessed | tf_op | source)
XLA Modules:
  0.0 508.4 jit_solution(8173655636678372656)
XLA Ops:
  0.6 0.0 copy-start
  0.6 0.6 copy-done
  1.3 25.3 %sums.1 = (f32[16,1,1024]{2,1,0:T(1,128)S(1)}, f32[16,1,1024]{2,1,0:T(1,128)S(1)}) custom-call(f32[16]{0:T(128)S(1)} %copy-done, f32[16,256,1024]{2,1,0:T(8,128)} %w_ref.2, f32[16,256,1024]{2,1,0:T(8,128)} %avg_ref.2, f32[16,256,1024]{2,1,0:T(8,128)} %w_ref.3, f32[16,256,1024]{2,1,0:T(8,128)} %avg_ref.3), custom_call_target="tpu_custom_call" | custom-call | flops 41943040 | bytes 67108864 | tf_op jit(solution)/shard_map/sums/pallas_call | solution.py:32
  26.6 0.1 pad_maximum_fusion
  26.7 0.7 copy.24
  27.4 7.3 %all-to-all-start = ((f32[8,32,128]{2,1,0:T(8,128)}), f32[8,32,128]{2,1,0:T(8,128)S(1)}, u32[]{:S(2)}, u32[]{:S(2)}) async-start(f32[8,32,128]{2,1,0:T(8,128)} %bitcast.23), calls=%async_computation | async-start | bytes 262144 | tf_op jit(solution)/shard_map/all_to_all | solution.py:111
  34.6 0.0 copy-done.2
  34.7 0.0 copy-done.3
  34.7 42.7 %all-gather.1 = bf16[8192,16]{0,1:T(8,128)(2,1)S(1)} all-gather(bf16[256,16]{0,1:T(8,128)(2,1)S(1)} %multiply_convert_fusion), channel_id=3, replica_groups=mesh['owner'=4,'rows'=8] {'rows','owner'}, dimensions={0}, use_global_device_ids=true | all-gather | bytes 270336 | tf_op jit(solution)/shard_map/all_gather | solution.py:105
  77.4 0.0 all-to-all-done
  77.4 30.5 %all-gather = f32[256,128]{1,0:T(8,128)S(1)} all-gather(f32[32,128]{1,0:T(8,128)S(1)} %get-tuple-element.18), channel_id=2, replica_groups=mesh['owner'=4,'rows'=8] {'rows'}, dimensions={0}, use_global_device_ids=true | all-gather | bytes 147456 | tf_op jit(solution)/shard_map/all_gather | solution.py:114
  108.0 0.1 copy.18
  108.1 18.9 %narrow.3 = bf16[8,16,256,128]{3,2,1,0:T(8,128)(2,1)} custom-call(f32[16]{0:T(128)S(1)} %copy-done.1, f32[16,256,1024]{2,1,0:T(8,128)} %w_ref.3, f32[16,256,1024]{2,1,0:T(8,128)} %avg_ref.3, f32[16,1,1024]{2,1,0:T(1,128)S(1)} %get-tuple-element.13.inverse_ref), custom_call_target="tpu_custom_call" | custom-call | flops 20971520 | bytes 41943040 | tf_op jit(solution)/shard_map/narrow/pallas_call | solution.py:59
  127.0 5.0 all-to-all-start.2
  132.1 18.9 %narrow.2 = bf16[8,16,256,128]{3,2,1,0:T(8,128)(2,1)} custom-call(f32[16]{0:T(128)S(1)} %copy-done.1, f32[16,256,1024]{2,1,0:T(8,128)} %w_ref.2, f32[16,256,1024]{2,1,0:T(8,128)} %avg_ref.2, f32[16,1,1024]{2,1,0:T(1,128)S(1)} %get-tuple-element.14.inverse_ref), custom_call_target="tpu_custom_call" | custom-call | flops 20971520 | bytes 41943040 | tf_op jit(solution)/shard_map/narrow/pallas_call | solution.py:59
  151.0 158.5 %all-to-all-done.2.in_ref = bf16[8,16,256,128]{3,2,1,0:T(8,128)(2,1)} async-done(((bf16[8,16,256,128]{3,2,1,0:T(8,128)(2,1)}), bf16[8,16,256,128]{3,2,1,0:T(8,128)(2,1)}, u32[]{:S(2)}, u32[]{:S(2)}) %all-to-all-start.2) | async-done | bytes 8388640 | tf_op jit(solution)/shard_map/all_to_all | solution.py:124
  309.5 4.9 all-to-all-start.1
  314.5 0.2 copy.19
  314.6 0.1 copy.20
  314.8 0.8 copy.22
  315.6 0.6 fusion
  316.2 11.9 %unpack.3 = bf16[16,2048,128]{2,1,0:T(8,128)(2,1)} custom-call(bf16[8,16,256,128]{3,2,1,0:T(8,128)(2,1)} %all-to-all-done.2.in_ref), custom_call_target="tpu_custom_call" | custom-call | flops 4194304 | bytes 16777216 | tf_op jit(solution)/shard_map/unpack/pallas_call | solution.py:86
  328.0 168.5 %all-to-all-done.1.in_ref = bf16[8,16,256,128]{3,2,1,0:T(8,128)(2,1)} async-done(((bf16[8,16,256,128]{3,2,1,0:T(8,128)(2,1)}), bf16[8,16,256,128]{3,2,1,0:T(8,128)(2,1)}, u32[]{:S(2)}, u32[]{:S(2)}) %all-to-all-start.1) | async-done | bytes 8388640 | tf_op jit(solution)/shard_map/all_to_all | solution.py:124
  496.5 11.9 %unpack.2 = bf16[16,2048,128]{2,1,0:T(8,128)(2,1)} custom-call(bf16[8,16,256,128]{3,2,1,0:T(8,128)(2,1)} %all-to-all-done.1.in_ref), custom_call_target="tpu_custom_call" | custom-call | flops 4194304 | bytes 16777216 | tf_op jit(solution)/shard_map/unpack/pallas_call | solution.py:86
  (9 shorter events, 0.1 us)
Async XLA Ops:
  0.6 0.7 copy-start
  1.3 33.4 %copy-start.2 = (f32[256,16]{0,1:T(8,128)S(1)}, f32[256,16]{0,1:T(8,128)}, u32[]{:S(2)}) copy-start(f32[256,16]{0,1:T(8,128)} %param.12) | copy-start | bytes 49156
  1.3 33.4 %copy-start.3 = (f32[256]{0:T(256)S(1)}, f32[256]{0:T(256)}, u32[]{:S(2)}) copy-start(f32[256]{0:T(256)} %param.13) | copy-start | bytes 3076
  1.3 106.8 %copy-start.1 = (f32[16]{0:T(128)S(1)}, f32[16]{0:T(128)}, u32[]{:S(2)}) copy-start(f32[16]{0:T(128)} %share_ref.5) | copy-start | bytes 196
  27.4 50.0 %all-to-all-start = ((f32[8,32,128]{2,1,0:T(8,128)}), f32[8,32,128]{2,1,0:T(8,128)S(1)}, u32[]{:S(2)}, u32[]{:S(2)}) async-start(f32[8,32,128]{2,1,0:T(8,128)} %bitcast.23), calls=%async_computation | async-start | bytes 262144 | tf_op jit(solution)/shard_map/all_to_all | solution.py:111
  127.0 182.5 %all-to-all-start.2 = ((bf16[8,16,256,128]{3,2,1,0:T(8,128)(2,1)}), bf16[8,16,256,128]{3,2,1,0:T(8,128)(2,1)}, u32[]{:S(2)}, u32[]{:S(2)}) async-start(bf16[8,16,256,128]{3,2,1,0:T(8,128)(2,1)} %narrow.3), calls=%async_computation.2 | async-start | bytes 16777216 | tf_op jit(solution)/shard_map/all_to_all | solution.py:124
  309.5 187.0 %all-to-all-start.1 = ((bf16[8,16,256,128]{3,2,1,0:T(8,128)(2,1)}), bf16[8,16,256,128]{3,2,1,0:T(8,128)(2,1)}, u32[]{:S(2)}, u32[]{:S(2)}) async-start(bf16[8,16,256,128]{3,2,1,0:T(8,128)(2,1)} %narrow.2), calls=%async_computation.1 | async-start | bytes 16777216 | tf_op jit(solution)/shard_map/all_to_all | solution.py:124

commit v2 on v1

v2 whole, which is shorter than its diff:
```python
import functools

import jax
import jax.numpy as jnp
from jax import lax
from jax.experimental import pallas as pl
from jax.experimental.pallas import tpu as pltpu
from jax.sharding import PartitionSpec as P

F32 = jnp.float32
BF16 = jnp.bfloat16


def params():
    return pltpu.CompilerParams(dimension_semantics=("arbitrary",), vmem_limit_bytes=48 * 2**20)


def mixed(share_ref, expert, w, avg):
    share = share_ref[expert]
    return share * w + (1.0 - share) * avg


def sums_kernel(share_ref, wg_ref, ag_ref, wu_ref, au_ref, gate_ref, up_ref):
    expert = pl.program_id(0)
    for w_ref, avg_ref, out_ref in ((wg_ref, ag_ref, gate_ref), (wu_ref, au_ref, up_ref)):
        fresh = mixed(share_ref, expert, w_ref[0], avg_ref[0])
        out_ref[0] = jnp.sum(fresh * fresh, axis=0, keepdims=True)


def sums(share, *arrays):
    experts, rows, width = arrays[0].shape
    block = pl.BlockSpec((1, rows, width), lambda e: (e, 0, 0))
    total = pl.BlockSpec((1, 1, width), lambda e: (e, 0, 0))
    return pl.pallas_call(
        sums_kernel,
        grid=(experts,),
        in_specs=[pl.BlockSpec(memory_space=pltpu.SMEM)] + [block] * 4,
        out_specs=[total] * 2,
        out_shape=[jax.ShapeDtypeStruct((experts, 1, width), F32)] * 2,
        compiler_params=params(),
        cost_estimate=pl.CostEstimate(
            flops=10 * experts * rows * width, bytes_accessed=16 * experts * rows * width, transcendentals=0
        ),
        name="sums",
    )(share, *arrays)


def narrow_kernel(first, share_ref, w_ref, avg_ref, inverse_ref, *refs):
    out_ref = refs[-1]
    expert = first + pl.program_id(0)
    parts, _, _, columns = out_ref.shape
    for part in range(parts):
        cut = slice(part * columns, (part + 1) * columns)
        fresh = mixed(share_ref, expert, w_ref[0, :, cut], avg_ref[0, :, cut])
        out_ref[part, 0] = (fresh * inverse_ref[0, :, cut]).astype(BF16)


def narrow(share, w, avg, inverse, parts, first, count, total, at=0, buffer=()):
    _, rows, width = w.shape
    columns = width // parts
    block = pl.BlockSpec((1, rows, width), lambda e: (first + e, 0, 0))
    return pl.pallas_call(
        functools.partial(narrow_kernel, first),
        grid=(count,),
        in_specs=[
            pl.BlockSpec(memory_space=pltpu.SMEM),
            block,
            block,
            pl.BlockSpec((1, 1, width), lambda e: (first + e, 0, 0)),
        ]
        + [pl.BlockSpec(memory_space=pl.ANY)] * len(buffer),
        out_specs=pl.BlockSpec((parts, 1, rows, columns), lambda e: (0, at + e, 0, 0)),
        out_shape=jax.ShapeDtypeStruct((parts, total, rows, columns), BF16),
        input_output_aliases={4: 0} if buffer else {},
        compiler_params=params(),
        cost_estimate=pl.CostEstimate(
            flops=5 * count * rows * width, bytes_accessed=10 * count * rows * width, transcendentals=0
        ),
        name="narrow",
    )(share, w, avg, inverse, *buffer)


def unpack_kernel(in_ref, *refs):
    out_ref = refs[-1]
    parts, _, rows, _ = in_ref.shape
    for part in range(parts):
        out_ref[0, part * rows : (part + 1) * rows] = in_ref[part, 0]


def unpack(arrived, first, count, total, at=0, buffer=()):
    parts, _, rows, columns = arrived.shape
    moved = parts * count * rows * columns
    return pl.pallas_call(
        unpack_kernel,
        grid=(count,),
        in_specs=[pl.BlockSpec((parts, 1, rows, columns), lambda e: (0, first + e, 0, 0))]
        + [pl.BlockSpec(memory_space=pl.ANY)] * len(buffer),
        out_specs=pl.BlockSpec((1, parts * rows, columns), lambda e: (at + e, 0, 0)),
        out_shape=jax.ShapeDtypeStruct((total, parts * rows, columns), BF16),
        input_output_aliases={1: 0} if buffer else {},
        compiler_params=params(),
        cost_estimate=pl.CostEstimate(flops=moved, bytes_accessed=4 * moved, transcendentals=0),
        name="unpack",
    )(arrived, *buffer)


def exchange(packed, axes="rows"):
    return lax.all_to_all(packed, axes, split_axis=0, concat_axis=0, tiled=True)


def to_all(block, axes, members):
    return exchange(jnp.broadcast_to(block, (members,) + block.shape), axes)


def body(parts, owners, w_gate, avg_gate, w_up, avg_up, mix_share, router_weight, router_gain):
    experts, _, width = w_gate.shape

    part_router = (router_weight * router_gain[:, None]).astype(BF16).T
    gathered = to_all(part_router, ("rows", "owner"), parts * owners)

    partial_gate, partial_up = sums(mix_share, w_gate, avg_gate, w_up, avg_up)
    partial = jnp.concatenate([partial_gate, partial_up]).reshape(2 * experts, parts, width // parts)
    pieces = exchange(partial.transpose(1, 0, 2))
    scale = jnp.sqrt(jnp.sum(pieces, axis=0))
    scale_gate, scale_up = scale[:experts], scale[experts:]
    inverse = to_all(1.0 / scale, "rows", parts)
    inverse = inverse.transpose(1, 0, 2).reshape(2, experts, 1, width)
    inverse, gathered = lax.optimization_barrier((inverse, gathered))
    router_columns, router_rows = part_router.shape
    serve_router = (
        gathered.reshape(parts, owners, router_columns, router_rows)
        .transpose(1, 2, 0, 3)
        .reshape(owners * router_columns, parts * router_rows)
        .T
    )

    few = max(1, experts // 4)
    rest = experts - few
    packed_first = narrow(mix_share, w_gate, avg_gate, inverse[0], parts, 0, few, few)
    arrived_first = exchange(packed_first)
    packed = narrow(mix_share, w_gate, avg_gate, inverse[0], parts, few, rest, 2 * rest)
    packed = narrow(mix_share, w_up, avg_up, inverse[1], parts, 0, rest, 2 * rest, rest, (packed,))
    arrived = exchange(packed)
    packed_last = narrow(mix_share, w_up, avg_up, inverse[1], parts, rest, few, few)
    arrived_last = exchange(packed_last)

    serve_gate = unpack(arrived_first, 0, few, experts)
    serve_gate = unpack(arrived, 0, rest, experts, few, (serve_gate,))
    serve_up = unpack(arrived, rest, rest, experts)
    serve_up = unpack(arrived_last, 0, few, experts, rest, (serve_up,))
    return (serve_gate, serve_up, scale_gate, scale_up, serve_router)


def solution(mesh):
    parts, owners = mesh.shape["rows"], mesh.shape["owner"]
    matrix = P("owner", "rows", None)
    in_specs = (matrix, matrix, matrix, matrix, P("owner"), P("rows", "owner"), P("rows"))
    served = P("owner", None, "rows")
    out_specs = (served, served, P("owner", "rows"), P("owner", "rows"), P())

    def step(*arguments):
        return body(parts, owners, *arguments)

    return jax.shard_map(step, mesh=mesh, in_specs=in_specs, out_specs=out_specs, check_vma=False)
```

time: 510 us -> 459 us (0.900)
  blocking collectives: 73.2 us -> 14.4 us
    all_gather x2 -> x0, blocking collectives: 73.2 us -> none  [the longest x1 42.7 us: body(): gathered = lax.all_gather(part_router, ('rows', 'owner'), axis=0)]
    all_to_all x0 -> x1, blocking collectives: none -> 14.4 us  [exchange(): return lax.all_to_all(packed, axes, split_axis=0, concat_axis=0, tiled=True)]
    all_to_all x3 -> x5, waiting for transfers between devices: 327 us -> 330 us  [exchange(): return lax.all_to_all(packed, axes, split_axis=0, concat_axis=0, tiled=True)]
    all_to_all x3 -> x5, starting transfers between devices: 17.3 us -> 19.3 us  [exchange(): return lax.all_to_all(packed, axes, split_axis=0, concat_axis=0, tiled=True)]
    pallas_call x4 -> x8, Pallas kernels: 61.6 us -> 61.9 us  [the longest x4 37.7 us: narrow(): pl.pallas_call(functools.partial(narrow_kernel, first), grid=(count,), in...]
  transfers between devices with their start and end apart: 3 -> 5, of which waited for: 2 -> 5; matrix products, arithmetic and copies ran while one was open for 0% -> 0% of each run, Pallas kernels for 6% -> 12%
where the time goes in v2:
time: 459 us; the launch traced here: 458 us
  waiting for transfers between devices  330 us (72%)
  Pallas kernels  87.1 us (19%)
  starting transfers between devices  19.3 us (4%)
  blocking collectives  14.4 us (3%)
  local copies, waits for them, and re-layouts  6.36 us (1%)
    all_to_all x5, waiting for transfers between devices, exchange(): return lax.all_to_all(packed, axes, split_axis=0, concat_axis=0, tiled=True)  330 us
    pallas_call x4, Pallas kernels, narrow(): pl.pallas_call(functools.partial(narrow_kernel, first), grid=(count,), in...  37.7 us
    pallas_call x1, Pallas kernels, sums(): pl.pallas_call(sums_kernel, grid=(experts,), in_specs=[pl.BlockSpec(memor...  25.3 us
    pallas_call x4, Pallas kernels, unpack(): pl.pallas_call(unpack_kernel, grid=(count,), in_specs=[pl.BlockSpec((part...  24.2 us
    all_to_all x5, starting transfers between devices, exchange(): return lax.all_to_all(packed, axes, split_axis=0, concat_axis=0, tiled=True)  19.3 us
    all_to_all x1, blocking collectives, exchange(): return lax.all_to_all(packed, axes, split_axis=0, concat_axis=0, tiled=True)  14.4 us
  transfers between devices with their start and end apart: 5, of which 5 were waited for; matrix products, arithmetic and copies ran while one was open for 0% of the time, Pallas kernels for 12%

profile of v2, /device:TPU:0, one launch (start us, length us, event | category | flops | bytes accessed | tf_op | source)
XLA Modules:
  0.0 458.1 jit_solution(10803863745652029865)
XLA Ops:
  1.3 25.3 %sums.1 = (f32[16,1,1024]{2,1,0:T(1,128)S(1)}, f32[16,1,1024]{2,1,0:T(1,128)S(1)}) custom-call(f32[16]{0:T(128)S(1)} %copy-done.2, f32[16,256,1024]{2,1,0:T(8,128)} %w_ref.6, f32[16,256,1024]{2,1,0:T(8,128)} %avg_ref.6, f32[16,256,1024]{2,1,0:T(8,128)} %w_ref.7, f32[16,256,1024]{2,1,0:T(8,128)} %avg_ref.7), custom_call_target="tpu_custom_call" | custom-call | flops 41943040 | bytes 67108864 | tf_op jit(solution)/shard_map/sums/pallas_call | solution.py:34
  26.7 14.4 %all_to_all.30 = f32[8,32,128]{2,1,0:T(8,128)S(1)} all-to-all(f32[8,32,128]{2,1,0:T(8,128)S(1)} %bitcast.25), channel_id=1, replica_groups=mesh['owner'=4,'rows'=8] {'rows'}, dimensions={0} | all-to-all | bytes 262144 | tf_op jit(solution)/shard_map/all_to_all | solution.py:108
  41.8 3.4 all-to-all-start.1
  45.3 7.2 %all-to-all-done.1 = f32[8,32,128]{2,1,0:T(8,128)S(1)} async-done(((f32[8,32,128]{2,1,0:T(8,128)}), f32[8,32,128]{2,1,0:T(8,128)S(1)}, u32[]{:S(2)}, u32[]{:S(2)}) %all-to-all-start.1) | async-done | bytes 131104 | tf_op jit(solution)/shard_map/all_to_all | solution.py:108
  52.5 0.7 broadcast_in_dim.8
  53.2 2.6 all-to-all-start.2
  55.9 10.5 %all-to-all-done.2 = bf16[32,16,256]{2,1,0:T(8,128)(2,1)S(1)} async-done(((bf16[32,16,256]{2,1,0:T(8,128)(2,1)}), bf16[32,16,256]{2,1,0:T(8,128)(2,1)S(1)}, u32[]{:S(2)}, u32[]{:S(2)}) %all-to-all-start.2) | async-done | bytes 262176 | tf_op jit(solution)/shard_map/all_to_all | solution.py:108
  66.4 4.4 narrow.6
  70.8 1.3 copy-done.1
  72.1 3.6 all-to-all-start.4
  75.8 14.4 %narrow.4.refs_0_ = bf16[8,24,256,128]{3,2,1,0:T(8,128)(2,1)} custom-call(f32[16]{0:T(128)S(1)} %copy-done.3, f32[16,256,1024]{2,1,0:T(8,128)} %w_ref.6, f32[16,256,1024]{2,1,0:T(8,128)} %avg_ref.6, f32[16,1,1024]{2,1,0:T(1,128)S(1)} %get-tuple-element.13.inverse_ref), custom_call_target="tpu_custom_call" | custom-call | flops 15728640 | bytes 31457280 | tf_op jit(solution)/shard_map/narrow/pallas_call | solution.py:62
  90.2 14.4 %narrow.5 = bf16[8,24,256,128]{3,2,1,0:T(8,128)(2,1)} custom-call(f32[16]{0:T(128)S(1)} %copy-done.3, f32[16,256,1024]{2,1,0:T(8,128)} %w_ref.7, f32[16,256,1024]{2,1,0:T(8,128)} %avg_ref.7, f32[16,1,1024]{2,1,0:T(1,128)S(1)} %get-tuple-element.14.inverse_ref, bf16[8,24,256,128]{3,2,1,0:T(8,128)(2,1)} %narrow.4.refs_0_), custom_call_target="tpu_custom_call", output_to_operand_aliasing={{}: (4, {})} | custom-call | flops 15728640 | bytes 31457280 | tf_op jit(solution)/shard_map/narrow/pallas_call | solution.py:62
  104.6 19.6 %all-to-all-done.4.in_ref = bf16[8,4,256,128]{3,2,1,0:T(8,128)(2,1)S(1)} async-done(((bf16[8,4,256,128]{3,2,1,0:T(8,128)(2,1)}), bf16[8,4,256,128]{3,2,1,0:T(8,128)(2,1)S(1)}, u32[]{:S(2)}, u32[]{:S(2)}) %all-to-all-start.4) | async-done | bytes 2097184 | tf_op jit(solution)/shard_map/all_to_all | solution.py:108
  124.3 5.4 %all-to-all-start.3 = ((bf16[8,24,256,128]{3,2,1,0:T(8,128)(2,1)}), bf16[8,24,256,128]{3,2,1,0:T(8,128)(2,1)}, u32[]{:S(2)}, u32[]{:S(2)}) async-start(bf16[8,24,256,128]{3,2,1,0:T(8,128)(2,1)} %narrow.5), calls=%async_computation.3 | async-start | bytes 25165824 | tf_op jit(solution)/shard_map/all_to_all | solution.py:108
  129.6 4.4 narrow.7
  134.1 1.4 copy-done
  135.4 266.7 %all-to-all-done.3.in_ref = bf16[8,24,256,128]{3,2,1,0:T(8,128)(2,1)} async-done(((bf16[8,24,256,128]{3,2,1,0:T(8,128)(2,1)}), bf16[8,24,256,128]{3,2,1,0:T(8,128)(2,1)}, u32[]{:S(2)}, u32[]{:S(2)}) %all-to-all-start.3) | async-done | bytes 12582944 | tf_op jit(solution)/shard_map/all_to_all | solution.py:108
  402.1 4.4 all-to-all-start.5
  407.2 0.8 copy.19
  408.0 1.9 unpack.4.refs_0_
  410.0 9.2 %unpack.6.refs_0_ = bf16[16,2048,128]{2,1,0:T(8,128)(2,1)} custom-call(bf16[8,24,256,128]{3,2,1,0:T(8,128)(2,1)} %all-to-all-done.3.in_ref), custom_call_target="tpu_custom_call" | custom-call | flops 3145728 | bytes 12582912 | tf_op jit(solution)/shard_map/unpack/pallas_call | solution.py:93
  419.2 9.2 %unpack.5 = bf16[16,2048,128]{2,1,0:T(8,128)(2,1)} custom-call(bf16[8,24,256,128]{3,2,1,0:T(8,128)(2,1)} %all-to-all-done.3.in_ref, bf16[16,2048,128]{2,1,0:T(8,128)(2,1)} %unpack.4.refs_0_), custom_call_target="tpu_custom_call", output_to_operand_aliasing={{}: (1, {})} | custom-call | flops 3145728 | bytes 12582912 | tf_op jit(solution)/shard_map/unpack/pallas_call | solution.py:93
  428.4 25.8 %all-to-all-done.5.in_ref = bf16[8,4,256,128]{3,2,1,0:T(8,128)(2,1)} async-done(((bf16[8,4,256,128]{3,2,1,0:T(8,128)(2,1)}), bf16[8,4,256,128]{3,2,1,0:T(8,128)(2,1)}, u32[]{:S(2)}, u32[]{:S(2)}) %all-to-all-start.5) | async-done | bytes 2097184 | tf_op jit(solution)/shard_map/all_to_all | solution.py:108
  454.3 3.8 unpack.7
  (20 shorter events, 2.4 us)
Async XLA Ops:
  0.6 0.7 copy-start.2
  1.3 43.9 %copy-start.4 = (f32[256,16]{0,1:T(8,128)S(1)}, f32[256,16]{0,1:T(8,128)}, u32[]{:S(2)}) copy-start(f32[256,16]{0,1:T(8,128)} %param.12) | copy-start | bytes 49156
  1.3 43.9 %copy-start.5 = (f32[256]{0:T(256)S(1)}, f32[256]{0:T(256)}, u32[]{:S(2)}) copy-start(f32[256]{0:T(256)} %param.13) | copy-start | bytes 3076
  1.3 65.1 %copy-start.3 = (f32[16]{0:T(128)S(1)}, f32[16]{0:T(128)}, u32[]{:S(2)}) copy-start(f32[16]{0:T(128)} %share_ref.9) | copy-start | bytes 196
  41.8 10.7 %all-to-all-start.1 = ((f32[8,32,128]{2,1,0:T(8,128)}), f32[8,32,128]{2,1,0:T(8,128)S(1)}, u32[]{:S(2)}, u32[]{:S(2)}) async-start(f32[8,32,128]{2,1,0:T(8,128)} %broadcast_in_dim.7), calls=%async_computation.1 | async-start | bytes 262144 | tf_op jit(solution)/shard_map/all_to_all | solution.py:108
  53.2 13.2 %all-to-all-start.2 = ((bf16[32,16,256]{2,1,0:T(8,128)(2,1)}), bf16[32,16,256]{2,1,0:T(8,128)(2,1)S(1)}, u32[]{:S(2)}, u32[]{:S(2)}) async-start(bf16[32,16,256]{2,1,0:T(8,128)(2,1)} %broadcast_in_dim.8), calls=%async_computation.2 | async-start | bytes 524288 | tf_op jit(solution)/shard_map/all_to_all | solution.py:108
  70.8 1.3 copy-start.1
  72.1 52.1 %all-to-all-start.4 = ((bf16[8,4,256,128]{3,2,1,0:T(8,128)(2,1)}), bf16[8,4,256,128]{3,2,1,0:T(8,128)(2,1)S(1)}, u32[]{:S(2)}, u32[]{:S(2)}) async-start(bf16[8,4,256,128]{3,2,1,0:T(8,128)(2,1)} %copy-done.1), calls=%async_computation.4 | async-start | bytes 4194304 | tf_op jit(solution)/shard_map/all_to_all | solution.py:108
  124.3 277.9 %all-to-all-start.3 = ((bf16[8,24,256,128]{3,2,1,0:T(8,128)(2,1)}), bf16[8,24,256,128]{3,2,1,0:T(8,128)(2,1)}, u32[]{:S(2)}, u32[]{:S(2)}) async-start(bf16[8,24,256,128]{3,2,1,0:T(8,128)(2,1)} %narrow.5), calls=%async_computation.3 | async-start | bytes 25165824 | tf_op jit(solution)/shard_map/all_to_all | solution.py:108
  134.1 1.4 copy-start
  402.1 52.2 %all-to-all-start.5 = ((bf16[8,4,256,128]{3,2,1,0:T(8,128)(2,1)}), bf16[8,4,256,128]{3,2,1,0:T(8,128)(2,1)}, u32[]{:S(2)}, u32[]{:S(2)}) async-start(bf16[8,4,256,128]{3,2,1,0:T(8,128)(2,1)} %copy-done), calls=%async_computation.5 | async-start | bytes 4194304 | tf_op jit(solution)/shard_map/all_to_all | solution.py:108
